TPU v7x, 128 devices: a whole 4x4x4 slice. The times are simulated.
128 devices in a mesh: node: 8 (over x, core), dev: 16 (over y, z).
Axes of the slice: x: 4, y: 4, z: 4, core: 2. Of those that a mesh axis runs over, the one named last changes fastest.
Arguments:
- expert_hidden: bfloat16 [131072, 1536], P(('node', 'dev')), may hold values from -6 to 6
- expert_down: bfloat16 [128, 1536, 5120], P(('node', 'dev')), may hold values from -0.15625 to 0.15625
- shared_hidden: bfloat16 [16384, 1536], P(('node', 'dev')), may hold values from -6 to 6
- shared_down: bfloat16 [1536, 5120], P('dev'), may hold values from -0.15625 to 0.15625
- expert_ids: int32 [16384, 6], P(('node', 'dev')), may hold values from 0 to 127, as said below
- gates: float32 [16384, 6], P(('node', 'dev')), may hold values from 0.1 to 2
Outputs:
- combined: bfloat16 [16384, 5120], P(('node', 'dev'))
Inputs may be any that keep to these rules, and one draw needn't show every extreme that they name: `expert_ids`: each row names 6 different experts, two in each of three different groups, expert e lying in group e // 16. Among the 128 rows of one device every group is named by exactly 48 rows and no expert by more than 8 rows; some expert is named by exactly 8 rows of every device.
All inputs are finite; a program needn't handle non-finite values.
Results may differ from a plain program's by a relative error of at most 0.0047.
Values may be sent and summed in bfloat16 or wider, within the bound.
A program may use at most 128 MiB of HBM per device.

v0:
```python
import jax
import jax.numpy as jnp
from jax import lax
from jax.sharding import PartitionSpec as P


def earlier_counts(indicator):
    row_count = indicator.shape[0]
    earlier = (jnp.arange(row_count)[:, None] > jnp.arange(row_count)[None, :]).astype(jnp.float32)
    return jnp.dot(
        earlier, indicator, preferred_element_type=jnp.float32, precision=lax.Precision.HIGHEST
    )


def expert_positions(expert_ids, expert_count):
    labels = jnp.arange(expert_count, dtype=jnp.int32)
    chosen = (expert_ids[:, :, None] == labels).astype(jnp.float32)
    before = earlier_counts(jnp.sum(chosen, axis=1))
    return jnp.sum(chosen * before[:, None, :], axis=2).astype(jnp.int32)


def body(expert_hidden, expert_down, shared_hidden, shared_down, expert_ids, gates):
    node_count = lax.axis_size("node")
    members = lax.axis_size("dev")
    experts = node_count * members
    capacity = expert_hidden.shape[0] // experts
    model_width = expert_down.shape[2]
    token_count = shared_hidden.shape[0]
    width = expert_ids.shape[1]
    outputs = jnp.dot(expert_hidden, expert_down[0], preferred_element_type=jnp.float32).astype(
        jnp.bfloat16
    )
    shared = jnp.dot(
        shared_hidden,
        lax.all_gather(shared_down, "dev", axis=0, tiled=True),
        preferred_element_type=jnp.float32,
    )
    arrived = lax.all_to_all(
        outputs.reshape(experts, capacity, model_width),
        ("node", "dev"),
        split_axis=0,
        concat_axis=0,
        tiled=True,
    )
    arrived = arrived.reshape(experts * capacity, model_width)
    slot_index = expert_ids * capacity + expert_positions(expert_ids, experts)
    picked = jnp.take(arrived, slot_index.reshape(-1), axis=0).reshape(
        token_count, width, model_width
    )
    routed = jnp.sum(gates[:, :, None] * picked.astype(jnp.float32), axis=1)
    return (shared + routed).astype(jnp.bfloat16)


def solution(mesh):
    in_specs = (
        P(("node", "dev"), None),
        P(("node", "dev"), None, None),
        P(("node", "dev"), None),
        P("dev", None),
        P(("node", "dev"), None),
        P(("node", "dev"), None),
    )
    out_specs = P(("node", "dev"), None)
    return jax.shard_map(body, mesh=mesh, in_specs=in_specs, out_specs=out_specs, check_vma=False)
```

profile of v0, /device:TPU:1, one launch (start us, length us, event | category | flops | bytes accessed | tf_op | source)
XLA Modules:
  0.0 251.5 jit_solution(1105196342037328720)
XLA Ops:
  6.5 0.0 copy-start
  6.5 0.0 all-gather.2.cloned.1.call-start
  6.5 0.7 all-gather.2.cloned.1.call-update
  7.3 1.2 copy-done
  8.4 22.2 %convert_bitcast_fusion = bf16[128,8,5120]{2,1,0:T(8,128)(2,1)} fusion(bf16[1024,1536]{1,0:T(8,128)(2,1)S(1)} %copy-done, bf16[1,1536,5120]{2,1,0:T(8,128)(2,1)} %param.7), kind=kOutput, calls=%fused_computation.4 | convolution fusion | flops 16111370240 | bytes 29360128 | tf_op jit(solution)/shard_map/dot_general | solution.py:30
  30.6 0.0 copy-start.3
  30.6 0.0 copy-start.4
  30.6 11.9 %all-to-all-start = ((bf16[128,8,5120]{2,1,0:T(8,128)(2,1)}), bf16[128,8,5120]{2,1,0:T(8,128)(2,1)}, u32[]{:S(2)}, u32[]{:S(2)}) async-start(bf16[128,8,5120]{2,1,0:T(8,128)(2,1)} %convert_bitcast_fusion), calls=%async_computation | async-start | bytes 20971520 | tf_op jit(solution)/shard_map/all_to_all | solution.py:38
  42.5 0.0 copy-done.3
  42.5 0.2 convert_reduce_fusion
  42.7 0.2 fusion.5
  42.9 0.3 select_reduce_fusion
  43.2 0.1 copy.16
  43.3 0.1 reshape.54
  43.5 0.0 copy-done.4
  43.5 0.7 copy.14
  44.2 0.1 copy.15
  44.4 144.9 %all-to-all-done = bf16[128,8,5120]{2,1,0:T(8,128)(2,1)} async-done(((bf16[128,8,5120]{2,1,0:T(8,128)(2,1)}), bf16[128,8,5120]{2,1,0:T(8,128)(2,1)}, u32[]{:S(2)}, u32[]{:S(2)}) %all-to-all-start) | async-done | bytes 10485792 | tf_op jit(solution)/shard_map/all_to_all | solution.py:38
  189.3 20.3 %gather_fusion = bf16[768,5120]{1,0:T(8,128)(2,1)} fusion(bf16[1024,5120]{1,0:T(8,128)(2,1)} %bitcast.2, s32[1024]{0:T(1024)S(1)} %pad_clamp_fusion), kind=kCustom, calls=%fused_computation | custom fusion | bytes 15731712 | tf_op jit(solution)/shard_map/jit(_take)/gather | solution.py:47
  209.6 13.1 %gather.7 = bf16[128,6,5120]{2,1,0:T(8,128)(2,1)} reshape(bf16[768,5120]{1,0:T(8,128)(2,1)} %gather_fusion) | data formatting | bytes 15728640 | tf_op jit(solution)/shard_map/jit(_take)/gather | solution.py:47
  222.7 0.0 copy-start.2
  222.7 0.0 copy-start.1
  222.7 12.4 %multiply_reduce_fusion = f32[128,5120]{1,0:T(8,128)} fusion(bf16[128,6,5120]{2,1,0:T(8,128)(2,1)} %gather.7, f32[128,6]{1,0:T(8,128)} %copy.14, pred[128,6]{1,0:T(8,128)(4,1)S(1)} %copy.15), kind=kLoop, calls=%fused_computation.1 | loop fusion | flops 15073280 | bytes 10489600 | tf_op jit(solution)/shard_map/reduce_sum | solution.py:50
  235.1 0.0 all-gather.2.cloned.1.call-done
  235.1 0.0 copy-done.2
  235.1 9.5 %fusion.4 = bf16[128,5120]{1,0:T(8,128)(2,1)} fusion(f32[128,5120]{1,0:T(8,128)} %multiply_reduce_fusion, bf16[128,1536]{1,0:T(8,128)(2,1)S(1)} %copy-done.2, bf16[1536,5120]{1,0:T(8,128)(2,1)} %all-gather.2.cloned.1.call-done), kind=kOutput, calls=%fused_computation.6 | convolution fusion | flops 2014576640 | bytes 20054016 | tf_op jit(solution)/shard_map/dot_general | solution.py:33
  244.6 0.0 copy-done.1
  (3 shorter events, 0.0 us)
Async XLA Ops:
  6.5 1.9 copy-start
  6.5 228.6 %all-gather.2.cloned.1.call-start = ((), (), s32[]{:S(2)}) async-start(), calls=%async_computation.1 | async-start | bytes 16711680 | tf_op jit(solution)/shard_map/all_gather | solution.py:35
  30.6 11.9 %copy-start.3 = (s32[128,6]{0,1:T(8,128)S(1)}, s32[128,6]{0,1:T(8,128)}, u32[]{:S(2)}) copy-start(s32[128,6]{0,1:T(8,128)} %param.10) | copy-start | bytes 9220
  30.6 12.9 %copy-start.4 = (f32[128,6]{0,1:T(8,128)S(1)}, f32[128,6]{0,1:T(8,128)}, u32[]{:S(2)}) copy-start(f32[128,6]{0,1:T(8,128)} %param.11) | copy-start | bytes 9220
  30.6 158.7 %all-to-all-start = ((bf16[128,8,5120]{2,1,0:T(8,128)(2,1)}), bf16[128,8,5120]{2,1,0:T(8,128)(2,1)}, u32[]{:S(2)}, u32[]{:S(2)}) async-start(bf16[128,8,5120]{2,1,0:T(8,128)(2,1)} %convert_bitcast_fusion), calls=%async_computation | async-start | bytes 20971520 | tf_op jit(solution)/shard_map/all_to_all | solution.py:38
  222.7 12.4 %copy-start.2 = (bf16[128,1536]{1,0:T(8,128)(2,1)S(1)}, bf16[128,1536]{1,0:T(8,128)(2,1)}, u32[]{:S(2)}) copy-start(bf16[128,1536]{1,0:T(8,128)(2,1)} %param.8) | copy-start | bytes 1179652
  222.7 21.9 %copy-start.1 = (bf16[1024,1536]{1,0:T(8,128)(2,1)S(1)}, bf16[1024,1536]{1,0:T(8,128)(2,1)}, u32[]{:S(2)}) copy-start(bf16[1024,1536]{1,0:T(8,128)(2,1)} %param.6) | copy-start | bytes 9437188
Sparse Core Ops, SparseCore 0:
  9.5 213.9 all-gather.1
where the time goes:
time: 256 us; the launch traced here: 251 us
  waiting for transfers between devices  146 us (57%)
  local copies, waits for them, and re-layouts  35.7 us (14%)
  matrix products  31.9 us (12%)
  between operations  13.5 us (5%)
  other arithmetic  12.9 us (5%)
  starting transfers between devices  11.9 us (5%)
    all_to_all x1, waiting for transfers between devices, body(): lax.all_to_all(outputs.reshape(experts, capacity, model_width), ('node',...  145 us
    gather x2, local copies, waits for them, and re-layouts, body(): jnp.take(arrived, slot_index.reshape(-1), axis=0)  33.4 us
    dot_general x1, matrix products, body(): jnp.dot(expert_hidden, expert_down[0], preferred_element_type=jnp.float32)  22.2 us
    reduce_sum x1, other arithmetic, body(): routed = jnp.sum(gates[:, :, None] * picked.astype(jnp.float32), axis=1)  12.4 us
    all_to_all x1, starting transfers between devices, body(): lax.all_to_all(outputs.reshape(experts, capacity, model_width), ('node',...  11.9 us
    dot_general x1, matrix products, body(): jnp.dot(shared_hidden, lax.all_gather(shared_down, 'dev', axis=0, tiled=T...  9.5 us
  transfers between devices with their start and end apart: 2, of which 1 were waited for; matrix products, arithmetic and copies ran while one was open for 28% of the time, Pallas kernels for 0%

commit v1 on v0

v1 whole, which is shorter than its diff:
```python
import functools

import jax
import jax.numpy as jnp
from jax import lax
from jax.experimental import pallas as pl
from jax.experimental.pallas import tpu as pltpu
from jax.sharding import PartitionSpec as P

MESH = pl.DeviceIdType.MESH
BF = jnp.bfloat16
F32 = jnp.float32
NODES = 8
RING = 4
CAP = 8
EXPERTS = 128
TOK = 128
TOP = 6
EF = 1536
D = 5120
KS = 384
C = 256
HALF = D // 2
STEPS = HALF // C
SLOTS = 3
NODE_OFFSETS = ((1, 0), (3, 0), (2, 0), (1, 1), (3, 1), (2, 1), (0, 1))


def iota(shape, dim):
    return lax.broadcasted_iota(jnp.int32, shape, dim)


def dot(a, b):
    return jnp.dot(a, b, preferred_element_type=F32)


def kernel(
    hid_h, wd_h, sh_h, shz_h, sd_h, ids_ref, gates_ref, out_h,
    hid, wbuf, obuf, recv1, recv2, recv3, pbuf, wg, gbig, hrecv, grecv, gsend, outv,
    load_sem, w_sem, own_sem, init_send, init_recv, send1, rsem1, send2, rsem2, send3, rsem3, out_sem,
):
    n = lax.axis_index("node")
    d = lax.axis_index("dev")
    x, core = n // 2, n % 2
    y, z = d // RING, d % RING

    def node_at(offset):
        ox, oc = offset
        return ((x + ox) % RING) * 2 + (core + oc) % 2

    def along(kind, step):
        if kind == 0:
            to = (z + step) % RING
            return to, y * RING + to
        to = (y + step) % RING
        return to, to * RING + z

    mine = (z, y)

    def load_w(step, slot):
        for k in range(2):
            col = pl.multiple_of(k * HALF + step * C, C)
            yield pltpu.make_async_copy(wd_h.at[:, pl.ds(col, C)], wbuf.at[slot, k], w_sem.at[slot, k])

    hid_copy = pltpu.make_async_copy(hid_h, hid, load_sem)
    hid_copy.start()
    for copy in load_w(0, 0):
        copy.start()
    own_copies = (
        pltpu.make_async_copy(sd_h.at[:, pl.ds(0, HALF)], wg.at[0, z], own_sem.at[0]),
        pltpu.make_async_copy(sd_h.at[:, pl.ds(HALF, HALF)], wg.at[1, y], own_sem.at[1]),
        pltpu.make_async_copy(sh_h.at[:, pl.ds(pl.multiple_of(y * KS, KS), KS)], hrecv.at[0, y], own_sem.at[2]),
        pltpu.make_async_copy(shz_h.at[z], hrecv.at[1, z], own_sem.at[3]),
    )
    for copy in own_copies:
        copy.start()

    barrier = pltpu.get_barrier_semaphore()
    for offset in NODE_OFFSETS:
        pl.semaphore_signal(barrier, inc=1, device_id=(node_at(offset), d), device_id_type=MESH)
    for kind in range(2):
        for step in range(1, RING):
            pl.semaphore_signal(barrier, inc=1, device_id=(n, along(kind, step)[1]), device_id_type=MESH)
    pl.semaphore_wait(barrier, len(NODE_OFFSETS) + 2 * (RING - 1))

    def remote(src, dst, ssem, rsem, node, dev):
        pltpu.make_async_remote_copy(
            src_ref=src, dst_ref=dst, send_sem=ssem, recv_sem=rsem, device_id=(node, dev), device_id_type=MESH
        ).start()

    def take(ref, sem):
        pltpu.make_async_copy(ref, ref, sem).wait()

    for step in (1, 3, 2):
        to, dev = along(1, step)
        remote(sh_h.at[:, pl.ds(pl.multiple_of(to * KS, KS), KS)], hrecv.at[0, y], init_send.at[0], init_recv.at[0], n, dev)
        to, dev = along(0, step)
        remote(shz_h.at[to], hrecv.at[1, z], init_send.at[1], init_recv.at[1], n, dev)
    for step in (1, 3, 2):
        _, dev = along(0, step)
        remote(sd_h.at[:, pl.ds(0, HALF)], wg.at[0, z], init_send.at[2], init_recv.at[2], n, dev)
        _, dev = along(1, step)
        remote(sd_h.at[:, pl.ds(HALF, HALF)], wg.at[1, y], init_send.at[3], init_recv.at[3], n, dev)

    def gate_pieces():
        label = iota((EXPERTS, TOK), 0)
        chosen = jnp.zeros((EXPERTS, TOK), F32)
        weight = jnp.zeros((EXPERTS, TOK), F32)
        for k in range(TOP):
            hit = ids_ref[k:k + 1, :] == label
            chosen += jnp.where(hit, 1.0, 0.0)
            weight += jnp.where(hit, gates_ref[k:k + 1, :], 0.0)
        earlier = (iota((TOK, TOK), 0) < iota((TOK, TOK), 1)).astype(F32).astype(BF)
        place = dot(chosen.astype(BF), earlier)
        place = jnp.where(chosen > 0.5, place, 255.0)
        place = jnp.transpose(place).astype(BF)
        weight = jnp.transpose(weight).astype(BF)
        lanes = CAP * EXPERTS // RING
        row = iota((EXPERTS, lanes), 0)
        lane = iota((EXPERTS, lanes), 1)
        other, group = lane // (CAP * NODES), (lane // CAP) % NODES
        slot = (iota((TOK, lanes), 1) % CAP).astype(F32)
        for k in range(2):
            for target in range(RING):
                local = target * RING + other if k == 0 else other * RING + target
                spread = jnp.where(row == group * (RING * RING) + local, 1.0, 0.0).astype(BF)
                piece = jnp.where(dot(place, spread) == slot, dot(weight, spread), 0.0)
                gsend[k, target] = piece.astype(BF)
        for k in range(2):
            own = mine[1 - k]
            grecv[k, own] = gsend[k, own]
            for step in (1, 3, 2):
                to, dev = along(1 - k, step)
                remote(gsend.at[k, to], grecv.at[k, own], init_send.at[4 + k], init_recv.at[4 + k], n, dev)

    def widen_gates():
        for k in range(2):
            take(grecv.at[k, pl.ds(0, RING - 1)], init_recv.at[4 + k])
        lanes = CAP * EXPERTS // RING
        row = iota((lanes, RING * lanes), 0)
        lane = iota((lanes, RING * lanes), 1)
        same = (row // CAP == lane // (RING * CAP)) & (row % CAP == lane % CAP)
        part = (lane // CAP) % RING
        for target in range(RING):
            spread = jnp.where(same & (part == target), 1.0, 0.0).astype(BF)
            for k in range(2):
                gbig[k, pl.ds(target * TOK, TOK), :] = dot(grecv[k, target], spread).astype(BF)
        for k in range(2):
            take(hrecv.at[k, pl.ds(0, RING - 1)], init_recv.at[k])
            take(wg.at[k, pl.ds(0, RING - 1)], init_recv.at[2 + k])
        for copy in own_copies:
            copy.wait()

    hid_copy.wait()

    def multiply(step):
        slot = step % 2
        place = step % SLOTS
        for copy in load_w(step, slot):
            copy.wait()

        @pl.when(step + 1 < STEPS)
        def _():
            for copy in load_w(step + 1, (step + 1) % 2):
                copy.start()

        @pl.when(step >= SLOTS)
        def _():
            for k in range(2):
                take(obuf.at[place, k, pl.ds(0, NODES - 1)], send1.at[place, k])

        for k in range(2):
            for part in range(2):
                rows = part * 512
                o = dot(hid[rows:rows + 512, :], wbuf[slot, k])
                if k == 0:
                    o = jnp.concatenate(
                        [
                            o[b * 128 + yy * 32 + zz * 8:b * 128 + yy * 32 + zz * 8 + 8]
                            for b in range(4) for zz in range(RING) for yy in range(RING)
                        ],
                        axis=0,
                    )
                obuf[place, k, pl.ds(part * 4, 4)] = o.astype(BF).reshape(4, 128, C)
            for offset in NODE_OFFSETS:
                to = node_at(offset)
                remote(obuf.at[place, k, to], recv1.at[k, step, n], send1.at[place, k], rsem1.at[k, step], to, d)
            recv1[k, step, n] = obuf[place, k, n]

    def forward(step):
        for k in range(2):
            take(recv1.at[k, step, pl.ds(0, NODES - 1)], rsem1.at[k, step])
            for hop in (1, 3, 2):
                to, dev = along(k, hop)
                rows = pl.multiple_of(to * 32, 32)
                remote(recv1.at[k, step, :, pl.ds(rows, 32), :], recv2.at[k, step, mine[k]], send2.at[k, step], rsem2.at[k, step], n, dev)
            rows = pl.multiple_of(mine[k] * 32, 32)
            recv2[k, step, mine[k]] = recv1[k, step, :, pl.ds(rows, 32), :]

    def combine(step):
        for k in range(2):
            take(recv2.at[k, step, pl.ds(0, RING - 1)], rsem2.at[k, step])
            slots = recv2[k, step].reshape(1024, C)
            cols = pl.multiple_of(step * C, C)
            weights = wg[k, :, :, pl.ds(cols, C)].reshape(KS, C)
            part = dot(gbig[k], slots) + dot(hrecv[k].reshape(RING * TOK, KS), weights)
            pbuf[k, step] = part.astype(BF).reshape(RING, TOK, C)
            own = mine[1 - k]
            for hop in (1, 3, 2):
                to, dev = along(1 - k, hop)
                remote(pbuf.at[k, step, to], recv3.at[k, step, own], send3.at[k, step], rsem3.at[k, step], n, dev)
            recv3[k, step, own] = pbuf[k, step, own]

    def out_copy(k, step):
        col = pl.multiple_of(k * HALF + step * C, C)
        return pltpu.make_async_copy(outv.at[k, step], out_h.at[:, pl.ds(col, C)], out_sem.at[k, step])

    def finish(step):
        for k in range(2):
            take(recv3.at[k, step, pl.ds(0, RING - 1)], rsem3.at[k, step])
            total = recv3[k, step, 0].astype(F32)
            for j in range(1, RING):
                total += recv3[k, step, j].astype(F32)
            outv[k, step] = total.astype(BF)
            out_copy(k, step).start()

    def loop(i, carry):
        @pl.when(i < STEPS)
        def _():
            multiply(i)

        @pl.when(i == 0)
        def _():
            gate_pieces()

        @pl.when((i >= 1) & (i < STEPS + 1))
        def _():
            forward(i - 1)

        @pl.when(i == 1)
        def _():
            widen_gates()

        @pl.when((i >= 2) & (i < STEPS + 2))
        def _():
            combine(i - 2)

        @pl.when(i >= 3)
        def _():
            finish(i - 3)

        return carry

    lax.fori_loop(0, STEPS + 3, loop, 0)

    for k in range(2):
        take(hrecv.at[k, pl.ds(0, RING - 1)], init_send.at[k])
        take(wg.at[k, pl.ds(0, RING - 1)], init_send.at[2 + k])
        take(gsend.at[k, pl.ds(0, RING - 1)], init_send.at[4 + k])
        for place in range(SLOTS):
            take(obuf.at[place, k, pl.ds(0, NODES - 1)], send1.at[place, k])

    def drain(step, carry):
        for k in range(2):
            take(recv2.at[k, step, pl.ds(0, RING - 1)], send2.at[k, step])
            take(recv3.at[k, step, pl.ds(0, RING - 1)], send3.at[k, step])
            out_copy(k, step).wait()
        return carry

    lax.fori_loop(0, STEPS, drain, 0)


def body(expert_hidden, expert_down, shared_hidden, shared_down, expert_ids, gates):
    hidden_z = shared_hidden.reshape(TOK, RING, RING, 96).transpose(2, 0, 1, 3).reshape(RING, TOK, KS)
    anywhere = pl.BlockSpec(memory_space=pl.ANY)
    vmem = pl.BlockSpec(memory_space=pltpu.VMEM)
    dma = pltpu.SemaphoreType.DMA
    return pl.pallas_call(
        kernel,
        out_shape=jax.ShapeDtypeStruct((TOK, D), BF),
        in_specs=[anywhere] * 5 + [vmem] * 2,
        out_specs=anywhere,
        scratch_shapes=[
            pltpu.VMEM((1024, EF), BF),
            pltpu.VMEM((2, 2, EF, C), BF),
            pltpu.VMEM((SLOTS, 2, NODES, 128, C), BF),
            pltpu.VMEM((2, STEPS, NODES, 128, C), BF),
            pltpu.VMEM((2, STEPS, RING, NODES, 32, C), BF),
            pltpu.VMEM((2, STEPS, RING, TOK, C), BF),
            pltpu.VMEM((2, STEPS, RING, TOK, C), BF),
            pltpu.VMEM((2, RING, 96, HALF), BF),
            pltpu.VMEM((2, RING * TOK, 1024), BF),
            pltpu.VMEM((2, RING, TOK, KS), BF),
            pltpu.VMEM((2, RING, TOK, 256), BF),
            pltpu.VMEM((2, RING, TOK, 256), BF),
            pltpu.VMEM((2, STEPS, TOK, C), BF),
            dma,
            dma((2, 2)),
            dma((4,)),
            dma((6,)),
            dma((6,)),
            dma((SLOTS, 2)),
            dma((2, STEPS)),
            dma((2, STEPS)),
            dma((2, STEPS)),
            dma((2, STEPS)),
            dma((2, STEPS)),
            dma((2, STEPS)),
        ],
        compiler_params=pltpu.CompilerParams(
            collective_id=0, has_side_effects=True, vmem_limit_bytes=64 * 1024 * 1024 - 65536
        ),
        name="combine",
    )(
        expert_hidden,
        expert_down.reshape(EF, D),
        shared_hidden,
        hidden_z,
        shared_down,
        expert_ids.T,
        gates.T,
    )


def solution(mesh):
    in_specs = (
        P(("node", "dev"), None),
        P(("node", "dev"), None, None),
        P(("node", "dev"), None),
        P("dev", None),
        P(("node", "dev"), None),
        P(("node", "dev"), None),
    )
    out_specs = P(("node", "dev"), None)
    return jax.shard_map(body, mesh=mesh, in_specs=in_specs, out_specs=out_specs, check_vma=False)
```

time: 256 us -> 154 us (0.60); the launches traced: 251 us -> 154 us
  Pallas kernels: 0 us -> 150 us
  waiting for transfers between devices: 146 us -> 0 us
  matrix products: 31.9 us -> 0 us
  local copies, waits for them, and re-layouts: 35.7 us -> 4.62 us
  between operations: 13.5 us -> 0.03 us
  other arithmetic: 12.9 us -> 0 us
  starting transfers between devices: 11.9 us -> 0 us
    pallas_call x0 -> x1, Pallas kernels: none -> 150 us  [body(): pl.pallas_call(kernel, out_shape=jax.ShapeDtypeStruct((TOK, D), BF), in_s...]
    all_to_all x1 -> x0, waiting for transfers between devices: 145 us -> none  [body(): lax.all_to_all(outputs.reshape(experts, capacity, model_width), ('node',...]
    gather x2 -> x0, local copies, waits for them, and re-layouts: 33.4 us -> none  [body(): jnp.take(arrived, slot_index.reshape(-1), axis=0)]
    dot_general x3 -> x0, matrix products: 31.9 us -> none  [the longest x1 22.2 us: body(): jnp.dot(expert_hidden, expert_down[0], preferred_element_type=jnp.float32)]
    reduce_sum x3 -> x0, other arithmetic: 12.8 us -> none  [the longest x1 12.4 us: body(): routed = jnp.sum(gates[:, :, None] * picked.astype(jnp.float32), axis=1)]
    all_to_all x1 -> x0, starting transfers between devices: 11.9 us -> none  [body(): lax.all_to_all(outputs.reshape(experts, capacity, model_width), ('node',...]
  transfers between devices with their start and end apart: 2 -> 0, of which waited for: 1 -> 0; matrix products, arithmetic and copies ran while one was open for 28% -> 0% of each run, Pallas kernels for 0% -> 0%
where the time goes in v1:
time: 154 us
  Pallas kernels  150 us (97%)
  local copies, waits for them, and re-layouts  4.62 us (3%)
    pallas_call x1, Pallas kernels, body(): pl.pallas_call(kernel, out_shape=jax.ShapeDtypeStruct((TOK, D), BF), in_s...  150 us
    unnamed x2, local copies, waits for them, and re-layouts  3.67 us

profile of v1, /device:TPU:1, one launch (start us, length us, event | category | flops | bytes accessed | tf_op | source)
XLA Modules:
  0.0 154.2 jit_solution(14137008172300044903)
XLA Ops:
  0.0 1.2 copy.8
  1.3 0.9 copy.10.shz_h
  2.2 149.5 %combine.1 = bf16[128,5120]{1,0:T(8,128)(2,1)} custom-call(bf16[1024,1536]{1,0:T(8,128)(2,1)} %hid_h.1, bf16[1536,5120]{1,0:T(8,128)(2,1)} %bitcast.7, bf16[128,1536]{1,0:T(8,128)(2,1)} %sh_h.1, bf16[4,128,384]{2,1,0:T(8,128)(2,1)} %copy.10.shz_h, bf16[96,5120]{1,0:T(8,128)(2,1)} %sd_h.1, s32[6,128]{1,0:T(8,128)} %bitcast.10, f32[6,128]{1,0:T(8,128)} %bitcast.11), custom_call_target="tpu_custom_call" | custom-call | tf_op jit(solution)/shard_map/combine/pallas_call | solution.py:278
  151.7 2.5 %copy.12 = bf16[128,5120]{1,0:T(8,128)(2,1)} copy(bf16[128,5120]{1,0:T(8,128)(2,1)} %combine.1) | data formatting | bytes 2621440
  (1 shorter events, 0.0 us)

commit v2 on v1

v2 whole, which is shorter than its diff:
```python
import functools

import jax
import jax.numpy as jnp
from jax import lax
from jax.experimental import pallas as pl
from jax.experimental.pallas import tpu as pltpu
from jax.sharding import PartitionSpec as P

MESH = pl.DeviceIdType.MESH
BF = jnp.bfloat16
F32 = jnp.float32
NODES = 8
RING = 4
CAP = 8
EXPERTS = 128
TOK = 128
TOP = 6
EF = 1536
D = 5120
KS = 384
C = 128
WIDE = 256
PARTS = WIDE // C
HALF = D // 2
STEPS = HALF // C
ROUNDS = HALF // WIDE
AHEAD = 2
SLOTS = AHEAD + 2
NODE_OFFSETS = ((1, 0), (3, 0), (2, 0), (1, 1), (3, 1), (2, 1), (0, 1))


def iota(shape, dim):
    return lax.broadcasted_iota(jnp.int32, shape, dim)


def dot(a, b):
    return jnp.dot(a, b, preferred_element_type=F32)


def kernel(
    hid_h, wd_h, sh_h, sd_h, ids_h, gates_h, out_ref,
    hid, sh_ref, ids_ref, gates_ref, wbuf, obuf, recv1, recv2, recv3, pbuf, wg, gbig, hrecv, grecv, hsend, gsend,
    load_sem, w_sem, own_sem, init_send, init_recv, send1, rsem1, send2, rsem2, send3, rsem3,
):
    n = lax.axis_index("node")
    d = lax.axis_index("dev")
    x, core = n // 2, n % 2
    y, z = d // RING, d % RING

    def node_at(offset):
        ox, oc = offset
        return ((x + ox) % RING) * 2 + (core + oc) % 2

    def along(kind, step):
        if kind == 0:
            to = (z + step) % RING
            return to, y * RING + to
        to = (y + step) % RING
        return to, to * RING + z

    mine = (z, y)

    def load_w(step, slot):
        for k in range(2):
            col = pl.multiple_of(k * HALF + step * WIDE, WIDE)
            yield pltpu.make_async_copy(wd_h.at[:, pl.ds(col, WIDE)], wbuf.at[slot, k], w_sem.at[slot, k])

    hid_copy = pltpu.make_async_copy(hid_h, hid, load_sem)
    hid_copy.start()
    for copy in load_w(0, 0):
        copy.start()
    small_copies = (
        pltpu.make_async_copy(sh_h, sh_ref, own_sem.at[2]),
        pltpu.make_async_copy(ids_h, ids_ref, own_sem.at[3]),
        pltpu.make_async_copy(gates_h, gates_ref, own_sem.at[4]),
    )
    own_copies = (
        pltpu.make_async_copy(sd_h.at[:, pl.ds(0, HALF)], wg.at[0, z], own_sem.at[0]),
        pltpu.make_async_copy(sd_h.at[:, pl.ds(HALF, HALF)], wg.at[1, y], own_sem.at[1]),
    )
    for copy in small_copies + own_copies:
        copy.start()

    barrier = pltpu.get_barrier_semaphore()
    for offset in NODE_OFFSETS:
        pl.semaphore_signal(barrier, inc=1, device_id=(node_at(offset), d), device_id_type=MESH)
    for kind in range(2):
        for step in range(1, RING):
            pl.semaphore_signal(barrier, inc=1, device_id=(n, along(kind, step)[1]), device_id_type=MESH)
    pl.semaphore_wait(barrier, len(NODE_OFFSETS) + 2 * (RING - 1))

    def remote(src, dst, ssem, rsem, node, dev):
        pltpu.make_async_remote_copy(
            src_ref=src, dst_ref=dst, send_sem=ssem, recv_sem=rsem, device_id=(node, dev), device_id_type=MESH
        ).start()

    def take(ref, sem):
        pltpu.make_async_copy(ref, ref, sem).wait()

    def set_up():
        for step in (1, 3, 2):
            _, dev = along(0, step)
            remote(sd_h.at[:, pl.ds(0, HALF)], wg.at[0, z], init_send.at[2], init_recv.at[2], n, dev)
            _, dev = along(1, step)
            remote(sd_h.at[:, pl.ds(HALF, HALF)], wg.at[1, y], init_send.at[3], init_recv.at[3], n, dev)
        for copy in small_copies:
            copy.wait()
        for target in range(RING):
            hsend[0, target] = sh_ref[:, target * KS:(target + 1) * KS]
            hsend[1, target] = jnp.concatenate(
                [sh_ref[:, (other * RING + target) * 96:(other * RING + target + 1) * 96] for other in range(RING)], axis=1
            )
        for k in range(2):
            own = mine[1 - k]
            hrecv[k, own] = hsend[k, own]
            for step in (1, 3, 2):
                to, dev = along(1 - k, step)
                remote(hsend.at[k, to], hrecv.at[k, own], init_send.at[k], init_recv.at[k], n, dev)

    def gate_pieces():
        label = iota((EXPERTS, TOK), 0)
        chosen = jnp.zeros((EXPERTS, TOK), F32)
        weight = jnp.zeros((EXPERTS, TOK), F32)
        for k in range(TOP):
            hit = ids_ref[k:k + 1, :] == label
            chosen += jnp.where(hit, 1.0, 0.0)
            weight += jnp.where(hit, gates_ref[k:k + 1, :], 0.0)
        earlier = (iota((TOK, TOK), 0) < iota((TOK, TOK), 1)).astype(F32).astype(BF)
        place = dot(chosen.astype(BF), earlier)
        place = jnp.where(chosen > 0.5, place, 255.0)
        place = jnp.transpose(place).astype(BF)
        weight = jnp.transpose(weight).astype(BF)
        lanes = CAP * EXPERTS // RING
        row = iota((EXPERTS, lanes), 0)
        lane = iota((EXPERTS, lanes), 1)
        other, group = lane // (CAP * NODES), (lane // CAP) % NODES
        slot = (iota((TOK, lanes), 1) % CAP).astype(F32)
        for k in range(2):
            for target in range(RING):
                local = target * RING + other if k == 0 else other * RING + target
                spread = jnp.where(row == group * (RING * RING) + local, 1.0, 0.0).astype(BF)
                piece = jnp.where(dot(place, spread) == slot, dot(weight, spread), 0.0)
                gsend[k, target] = piece.astype(BF)
        for k in range(2):
            own = mine[1 - k]
            grecv[k, own] = gsend[k, own]
            for step in (1, 3, 2):
                to, dev = along(1 - k, step)
                remote(gsend.at[k, to], grecv.at[k, own], init_send.at[4 + k], init_recv.at[4 + k], n, dev)

    def widen_gates():
        for k in range(2):
            take(grecv.at[k, pl.ds(0, RING - 1)], init_recv.at[4 + k])
        lanes = CAP * EXPERTS // RING
        row = iota((lanes, RING * lanes), 0)
        lane = iota((lanes, RING * lanes), 1)
        same = (row // CAP == lane // (RING * CAP)) & (row % CAP == lane % CAP)
        part = (lane // CAP) % RING
        for target in range(RING):
            spread = jnp.where(same & (part == target), 1.0, 0.0).astype(BF)
            for k in range(2):
                gbig[k, pl.ds(target * TOK, TOK), :] = dot(grecv[k, target], spread).astype(BF)
        for k in range(2):
            take(hrecv.at[k, pl.ds(0, RING - 1)], init_recv.at[k])
            take(wg.at[k, pl.ds(0, RING - 1)], init_recv.at[2 + k])
        for copy in own_copies:
            copy.wait()

    hid_copy.wait()

    def multiply(step):
        slot = step % 2
        place = step % SLOTS
        for copy in load_w(step, slot):
            copy.wait()

        @pl.when(step + 1 < ROUNDS)
        def _():
            for copy in load_w(step + 1, (step + 1) % 2):
                copy.start()

        @pl.when(step >= SLOTS)
        def _():
            for k in range(2):
                for h in range(PARTS):
                    take(obuf.at[place, k, h, pl.ds(0, NODES - 1)], send1.at[place, k, h])

        for k in range(2):
            for part in range(2):
                rows = part * 512
                o = dot(hid[rows:rows + 512, :], wbuf[slot, k])
                if k == 0:
                    o = jnp.concatenate(
                        [
                            o[b * 128 + yy * 32 + zz * 8:b * 128 + yy * 32 + zz * 8 + 8]
                            for b in range(4) for zz in range(RING) for yy in range(RING)
                        ],
                        axis=0,
                    )
                o = o.astype(BF)
                for h in range(PARTS):
                    obuf[place, k, h, pl.ds(part * 4, 4)] = o[:, h * C:(h + 1) * C].reshape(4, 128, C)
            for h in range(PARTS):
                small = step * PARTS + h
                for offset in NODE_OFFSETS:
                    to = node_at(offset)
                    remote(obuf.at[place, k, h, to], recv1.at[k, small, n], send1.at[place, k, h], rsem1.at[k, small], to, d)
                recv1[k, small, n] = obuf[place, k, h, n]

    def forward(k, step):
        take(recv1.at[k, step, pl.ds(0, NODES - 1)], rsem1.at[k, step])
        for hop in (1, 3, 2):
            to, dev = along(k, hop)
            rows = pl.multiple_of(to * 32, 32)
            remote(recv1.at[k, step, :, pl.ds(rows, 32), :], recv2.at[k, step, mine[k]], send2.at[k, step], rsem2.at[k, step], n, dev)
        rows = pl.multiple_of(mine[k] * 32, 32)
        recv2[k, step, mine[k]] = recv1[k, step, :, pl.ds(rows, 32), :]

    def combine(k, step):
        take(recv2.at[k, step, pl.ds(0, RING - 1)], rsem2.at[k, step])
        slots = recv2[k, step].reshape(1024, C)
        cols = pl.multiple_of(step * C, C)
        weights = wg[k, :, :, pl.ds(cols, C)].reshape(KS, C)
        part = dot(gbig[k], slots) + dot(hrecv[k].reshape(RING * TOK, KS), weights)
        pbuf[k, step] = part.astype(BF).reshape(RING, TOK, C)
        own = mine[1 - k]
        for hop in (1, 3, 2):
            to, dev = along(1 - k, hop)
            remote(pbuf.at[k, step, to], recv3.at[k, step, own], send3.at[k, step], rsem3.at[k, step], n, dev)
        recv3[k, step, own] = pbuf[k, step, own]

    def finish(k, step):
        take(recv3.at[k, step, pl.ds(0, RING - 1)], rsem3.at[k, step])
        total = recv3[k, step, 0].astype(F32)
        for j in range(1, RING):
            total += recv3[k, step, j].astype(F32)
        out_ref[:, pl.ds(pl.multiple_of(k * HALF + step * C, C), C)] = total.astype(BF)

    def stage(i, lag, act):
        @pl.when((i >= lag) & (i < ROUNDS + lag))
        def _():
            for k in range(2):
                for h in range(PARTS):
                    act(k, (i - lag) * PARTS + h)

    def loop(i, carry):
        @pl.when(i < ROUNDS)
        def _():
            multiply(i)

        @pl.when(i == 0)
        def _():
            set_up()
            gate_pieces()

        stage(i, AHEAD, forward)

        @pl.when(i == AHEAD + 1)
        def _():
            widen_gates()

        stage(i, AHEAD + 1, combine)
        stage(i, AHEAD + 2, finish)
        return carry

    lax.fori_loop(0, ROUNDS + AHEAD + 2, loop, 0)

    for k in range(2):
        take(hsend.at[k, pl.ds(0, RING - 1)], init_send.at[k])
        take(wg.at[k, pl.ds(0, RING - 1)], init_send.at[2 + k])
        take(gsend.at[k, pl.ds(0, RING - 1)], init_send.at[4 + k])
        for h in range(PARTS):
            for place in range(SLOTS):
                take(obuf.at[place, k, h, pl.ds(0, NODES - 1)], send1.at[place, k, h])

    def drain(step, carry):
        for k in range(2):
            take(recv2.at[k, step, pl.ds(0, RING - 1)], send2.at[k, step])
            take(recv3.at[k, step, pl.ds(0, RING - 1)], send3.at[k, step])
        return carry

    lax.fori_loop(0, STEPS, drain, 0)


def body(expert_hidden, expert_down, shared_hidden, shared_down, expert_ids, gates):
    anywhere = pl.BlockSpec(memory_space=pl.ANY)
    vmem = pl.BlockSpec(memory_space=pltpu.VMEM)
    dma = pltpu.SemaphoreType.DMA
    return pl.pallas_call(
        kernel,
        out_shape=pltpu.VMEM((TOK, D), BF),
        in_specs=[anywhere] * 6,
        out_specs=vmem,
        scratch_shapes=[
            pltpu.VMEM((1024, EF), BF),
            pltpu.VMEM((TOK, EF), BF),
            pltpu.VMEM((TOP, TOK), jnp.int32),
            pltpu.VMEM((TOP, TOK), F32),
            pltpu.VMEM((2, 2, EF, WIDE), BF),
            pltpu.VMEM((SLOTS, 2, PARTS, NODES, 128, C), BF),
            pltpu.VMEM((2, STEPS, NODES, 128, C), BF),
            pltpu.VMEM((2, STEPS, RING, NODES, 32, C), BF),
            pltpu.VMEM((2, STEPS, RING, TOK, C), BF),
            pltpu.VMEM((2, STEPS, RING, TOK, C), BF),
            pltpu.VMEM((2, RING, 96, HALF), BF),
            pltpu.VMEM((2, RING * TOK, 1024), BF),
            pltpu.VMEM((2, RING, TOK, KS), BF),
            pltpu.VMEM((2, RING, TOK, 256), BF),
            pltpu.VMEM((2, RING, TOK, KS), BF),
            pltpu.VMEM((2, RING, TOK, 256), BF),
            dma,
            dma((2, 2)),
            dma((5,)),
            dma((6,)),
            dma((6,)),
            dma((SLOTS, 2, PARTS)),
            dma((2, STEPS)),
            dma((2, STEPS)),
            dma((2, STEPS)),
            dma((2, STEPS)),
            dma((2, STEPS)),
        ],
        compiler_params=pltpu.CompilerParams(
            collective_id=0, has_side_effects=True, vmem_limit_bytes=56 * 1024 * 1024
        ),
        name="combine",
    )(
        expert_hidden,
        expert_down.reshape(EF, D),
        shared_hidden,
        shared_down,
        expert_ids.T,
        gates.T,
    )


def solution(mesh):
    in_specs = (
        P(("node", "dev"), None),
        P(("node", "dev"), None, None),
        P(("node", "dev"), None),
        P("dev", None),
        P(("node", "dev"), None),
        P(("node", "dev"), None),
    )
    out_specs = P(("node", "dev"), None)
    return jax.shard_map(body, mesh=mesh, in_specs=in_specs, out_specs=out_specs, check_vma=False)
```

time: 154 us -> 139 us (0.903)
  Pallas kernels: 150 us -> 138 us
  local copies, waits for them, and re-layouts: 4.62 us -> 1.06 us
    pallas_call x1, Pallas kernels: 150 us -> 138 us  [body(): pl.pallas_call(kernel, out_shape=pltpu.VMEM((TOK, D), BF), in_specs=[anyw...]
    unnamed x2 -> x1, local copies, waits for them, and re-layouts: 3.67 us -> 1.06 us
where the time goes in v2:
time: 139 us
  Pallas kernels  138 us (99%)
    pallas_call x1, Pallas kernels, body(): pl.pallas_call(kernel, out_shape=pltpu.VMEM((TOK, D), BF), in_specs=[anyw...  138 us

profile of v2, /device:TPU:1, one launch (start us, length us, event | category | flops | bytes accessed | tf_op | source)
XLA Modules:
  0.0 138.8 jit_solution(10020850730697611769)
XLA Ops:
  0.0 137.7 %combine.1 = bf16[128,5120]{1,0:T(8,128)(2,1)S(1)} custom-call(bf16[1024,1536]{1,0:T(8,128)(2,1)} %hid_h.1, bf16[1536,5120]{1,0:T(8,128)(2,1)} %bitcast.3, bf16[128,1536]{1,0:T(8,128)(2,1)} %sh_h.1, bf16[96,5120]{1,0:T(8,128)(2,1)} %sd_h.1, s32[6,128]{1,0:T(8,128)} %bitcast.4, f32[6,128]{1,0:T(8,128)} %bitcast.5), custom_call_target="tpu_custom_call" | custom-call | tf_op jit(solution)/shard_map/combine/pallas_call | solution.py:290
  137.7 1.1 copy.8

commit v3 on v2

--- a/solution.py
+++ b/solution.py
@@ -23,9 +23,13 @@
 WIDE = 256
 PARTS = WIDE // C
 HALF = D // 2
-STEPS = HALF // C
-ROUNDS = HALF // WIDE
-AHEAD = 2
+XR = 2
+ROUNDS = HALF // WIDE - XR
+ALL = ROUNDS + XR
+LAST = ROUNDS - 1
+PACK = 48
+QUART = HALF // 2
+AHEAD = 3
 SLOTS = AHEAD + 2
 NODE_OFFSETS = ((1, 0), (3, 0), (2, 0), (1, 1), (3, 1), (2, 1), (0, 1))
 
@@ -41,7 +45,9 @@
 def kernel(
     hid_h, wd_h, sh_h, sd_h, ids_h, gates_h, out_ref,
     hid, sh_ref, ids_ref, gates_ref, wbuf, obuf, recv1, recv2, recv3, pbuf, wg, gbig, hrecv, grecv, hsend, gsend,
+    xbuf, xr1, xr2, xr3, xpart, abig, asend, arecv, place_back,
     load_sem, w_sem, own_sem, init_send, init_recv, send1, rsem1, send2, rsem2, send3, rsem3,
+    xs1, xq1, xs2, xq2, xs3, xq3, ash, arc,
 ):
     n = lax.axis_index("node")
     d = lax.axis_index("dev")
@@ -60,6 +66,9 @@
         return to, to * RING + z
 
     mine = (z, y)
+
+    def my_quart(base):
+        return pl.ds(pl.multiple_of(base + core * QUART, 128), QUART)
 
     def load_w(step, slot):
         for k in range(2):
@@ -76,8 +85,8 @@
         pltpu.make_async_copy(gates_h, gates_ref, own_sem.at[4]),
     )
     own_copies = (
-        pltpu.make_async_copy(sd_h.at[:, pl.ds(0, HALF)], wg.at[0, z], own_sem.at[0]),
-        pltpu.make_async_copy(sd_h.at[:, pl.ds(HALF, HALF)], wg.at[1, y], own_sem.at[1]),
+        pltpu.make_async_copy(sd_h.at[:, my_quart(0)], wg.at[0, z, :, my_quart(0)], own_sem.at[0]),
+        pltpu.make_async_copy(sd_h.at[:, my_quart(HALF)], wg.at[1, y, :, my_quart(0)], own_sem.at[1]),
     )
     for copy in small_copies + own_copies:
         copy.start()
@@ -98,12 +107,14 @@
     def take(ref, sem):
         pltpu.make_async_copy(ref, ref, sem).wait()
 
-    def set_up():
+    def send_rows():
         for step in (1, 3, 2):
             _, dev = along(0, step)
-            remote(sd_h.at[:, pl.ds(0, HALF)], wg.at[0, z], init_send.at[2], init_recv.at[2], n, dev)
+            remote(sd_h.at[:, my_quart(0)], wg.at[0, z, :, my_quart(0)], init_send.at[2], init_recv.at[2], n, dev)
             _, dev = along(1, step)
-            remote(sd_h.at[:, pl.ds(HALF, HALF)], wg.at[1, y], init_send.at[3], init_recv.at[3], n, dev)
+            remote(sd_h.at[:, my_quart(HALF)], wg.at[1, y, :, my_quart(0)], init_send.at[3], init_recv.at[3], n, dev)
+
+    def set_up():
         for copy in small_copies:
             copy.wait()
         for target in range(RING):
@@ -129,6 +140,14 @@
         earlier = (iota((TOK, TOK), 0) < iota((TOK, TOK), 1)).astype(F32).astype(BF)
         place = dot(chosen.astype(BF), earlier)
         place = jnp.where(chosen > 0.5, place, 255.0)
+        named = jnp.sum(chosen.reshape(NODES, EXPERTS // NODES, TOK), axis=1) * 0.5
+        rank = dot(named.astype(BF), earlier)
+        rank = jnp.where(named > 0.5, rank, 255.0)
+        pick = jnp.concatenate(
+            [jnp.where(iota((PACK, TOK), 0).astype(F32) == rank[g:g + 1, :], 1.0, 0.0) for g in range(NODES)], axis=0
+        )
+        place_back[...] = jnp.transpose(pick).astype(BF)
+        pick = pick.astype(BF)
         place = jnp.transpose(place).astype(BF)
         weight = jnp.transpose(weight).astype(BF)
         lanes = CAP * EXPERTS // RING
@@ -142,6 +161,17 @@
                 spread = jnp.where(row == group * (RING * RING) + local, 1.0, 0.0).astype(BF)
                 piece = jnp.where(dot(place, spread) == slot, dot(weight, spread), 0.0)
                 gsend[k, target] = piece.astype(BF)
+        row = iota((EXPERTS, EXPERTS), 0)
+        lane = iota((EXPERTS, EXPERTS), 1)
+        slot = (iota((TOK, EXPERTS), 1) % CAP).astype(F32)
+        for g in range(NODES):
+            spread = jnp.where(row == g * (RING * RING) + lane // CAP, 1.0, 0.0).astype(BF)
+            piece = jnp.where(dot(place, spread) == slot, dot(weight, spread), 0.0).astype(BF)
+            asend[g] = dot(pick[g * PACK:(g + 1) * PACK], piece).astype(BF)
+        arecv[n] = asend[n]
+        for offset in NODE_OFFSETS:
+            to = node_at(offset)
+            remote(asend.at[to], arecv.at[n], ash, arc, to, d)
         for k in range(2):
             own = mine[1 - k]
             grecv[k, own] = gsend[k, own]
@@ -163,28 +193,107 @@
                 gbig[k, pl.ds(target * TOK, TOK), :] = dot(grecv[k, target], spread).astype(BF)
         for k in range(2):
             take(hrecv.at[k, pl.ds(0, RING - 1)], init_recv.at[k])
-            take(wg.at[k, pl.ds(0, RING - 1)], init_recv.at[2 + k])
+            take(wg.at[k, :, :, pl.ds(0, QUART)], init_recv.at[6 + k])
+
+    def share_rows():
         for copy in own_copies:
             copy.wait()
-
-    hid_copy.wait()
+        for k in range(2):
+            take(wg.at[k, pl.ds(0, RING - 1), :, pl.ds(0, QUART)], init_recv.at[2 + k])
+            half = wg.at[k, :, :, my_quart(0)]
+            remote(half, half, init_send.at[6 + k], init_recv.at[6 + k], x * 2 + 1 - core, d)
+
+    def widen_x():
+        take(arecv.at[pl.ds(0, NODES - 1)], arc)
+        row = iota((EXPERTS, 1024), 0)
+        lane = iota((EXPERTS, 1024), 1)
+        outer, inner, node = lane // 256, (lane // 64) % RING, (lane // CAP) % NODES
+        for k in range(2):
+            local = outer * RING + inner if k == 0 else inner * RING + outer
+            same = (row // CAP == local) & (row % CAP == lane % CAP)
+            for m in range(NODES):
+                spread = jnp.where(same & (node == m), 1.0, 0.0).astype(BF)
+                abig[k, m * PACK:(m + 1) * PACK, :] = dot(arecv[m], spread).astype(BF)
+
+    def x_multiply(xr):
+        for copy in load_w(ROUNDS + xr, xr):
+            copy.wait()
+        for copy in load_w(ROUNDS + 1 if xr == 0 else 2, 1 - xr):
+            copy.start()
+        for k in range(2):
+            for part in range(2):
+                rows = part * 512
+                o = dot(hid[rows:rows + 512, :], wbuf[xr, k])
+                pieces = []
+                for outer in range(RING):
+                    for inner in range(RING):
+                        yy, zz = (inner, outer) if k == 0 else (outer, inner)
+                        for b in range(4):
+                            at = b * 128 + yy * 32 + zz * 8
+                            pieces.append(o[at:at + 8])
+                o = jnp.concatenate(pieces, axis=0).astype(BF)
+                xbuf[k, xr, :, :, part * 32:(part + 1) * 32, :] = o.reshape(RING, RING, 32, WIDE)
+            for hop in (1, 3, 2):
+                to, dev = along(k, hop)
+                remote(xbuf.at[k, xr, to], xr1.at[k, xr, mine[k]], xs1.at[k, xr], xq1.at[k, xr], n, dev)
+            xr1[k, xr, mine[k]] = xbuf[k, xr, mine[k]]
+
+    def x_forward(xr):
+        for k in range(2):
+            take(xr1.at[k, xr, pl.ds(0, RING - 1)], xq1.at[k, xr])
+            own = mine[1 - k]
+            for hop in (1, 3, 2):
+                to, dev = along(1 - k, hop)
+                remote(xr1.at[k, xr, :, to], xr2.at[k, xr, own], xs2.at[k, xr], xq2.at[k, xr], n, dev)
+            xr2[k, xr, own] = xr1[k, xr, :, own]
+
+    def x_combine(xr):
+        for k in range(2):
+            take(xr2.at[k, xr, pl.ds(0, RING - 1)], xq2.at[k, xr])
+            part = dot(abig[k], xr2[k, xr].reshape(1024, WIDE))
+            xpart[k, xr] = part.astype(BF).reshape(NODES, PACK, WIDE)
+            for offset in NODE_OFFSETS:
+                to = node_at(offset)
+                remote(xpart.at[k, xr, to], xr3.at[k, xr, n], xs3.at[k, xr], xq3.at[k, xr], to, d)
+            xr3[k, xr, n] = xpart[k, xr, n]
+            weights = wg[k, :, :, (ROUNDS + xr) * WIDE:(ROUNDS + xr + 1) * WIDE].reshape(KS, WIDE)
+            send_part(k, ROUNDS + xr, 0, WIDE, ROUNDS + 1 + xr, dot(hrecv[k].reshape(RING * TOK, KS), weights))
+
+    def x_finish(xr):
+        for k in range(2):
+            take(xr3.at[k, xr, pl.ds(0, NODES - 1)], xq3.at[k, xr])
+            routed = dot(place_back[...], xr3[k, xr].reshape(NODES * PACK, WIDE))
+            finish(k, ROUNDS + xr, 0, WIDE, ROUNDS + 1 + xr, routed)
+
 
     def multiply(step):
+        first = isinstance(step, int)
         slot = step % 2
         place = step % SLOTS
         for copy in load_w(step, slot):
             copy.wait()
-
-        @pl.when(step + 1 < ROUNDS)
-        def _():
-            for copy in load_w(step + 1, (step + 1) % 2):
+        if first:
+            for copy in load_w(1 if step == 0 else ROUNDS, 1 - slot):
                 copy.start()
-
-        @pl.when(step >= SLOTS)
-        def _():
-            for k in range(2):
-                for h in range(PARTS):
-                    take(obuf.at[place, k, h, pl.ds(0, NODES - 1)], send1.at[place, k, h])
+        else:
+            @pl.when(step + 1 < ROUNDS)
+            def _():
+                for copy in load_w(step + 1, (step + 1) % 2):
+                    copy.start()
+
+            @pl.when(step >= SLOTS)
+            def _():
+                for k in range(2):
+                    take(obuf.at[place, k, pl.ds(0, NODES - 1)], send1.at[place, k, 0])
+
+        def send(k, lane, width, h):
+            cols = pl.ds(lane, width)
+            for offset in NODE_OFFSETS:
+                to = node_at(offset)
+                remote(
+                    obuf.at[place, k, to, :, cols], recv1.at[k, step, n, :, cols],
+                    send1.at[place, k, h], rsem1.at[k, step + h], to, d,
+                )
 
         for k in range(2):
             for part in range(2):
@@ -198,81 +307,132 @@
                         ],
                         axis=0,
                     )
-                o = o.astype(BF)
-                for h in range(PARTS):
-                    obuf[place, k, h, pl.ds(part * 4, 4)] = o[:, h * C:(h + 1) * C].reshape(4, 128, C)
-            for h in range(PARTS):
-                small = step * PARTS + h
-                for offset in NODE_OFFSETS:
-                    to = node_at(offset)
-                    remote(obuf.at[place, k, h, to], recv1.at[k, small, n], send1.at[place, k, h], rsem1.at[k, small], to, d)
-                recv1[k, small, n] = obuf[place, k, h, n]
-
-    def forward(k, step):
-        take(recv1.at[k, step, pl.ds(0, NODES - 1)], rsem1.at[k, step])
+                obuf[place, k, pl.ds(part * 4, 4)] = o.astype(BF).reshape(4, 128, WIDE)
+            if first:
+                send(k, 0, WIDE, 0)
+            else:
+                @pl.when(step < LAST)
+                def _():
+                    send(k, 0, WIDE, 0)
+
+                @pl.when(step == LAST)
+                def _():
+                    for h in range(PARTS):
+                        send(k, h * C, C, h)
+            recv1[k, step, n] = obuf[place, k, n]
+
+    def forward(k, step, lane, width, sem):
+        cols = pl.ds(lane, width)
+        take(recv1.at[k, step, pl.ds(0, NODES - 1), :, cols], rsem1.at[k, sem])
         for hop in (1, 3, 2):
             to, dev = along(k, hop)
             rows = pl.multiple_of(to * 32, 32)
-            remote(recv1.at[k, step, :, pl.ds(rows, 32), :], recv2.at[k, step, mine[k]], send2.at[k, step], rsem2.at[k, step], n, dev)
+            remote(
+                recv1.at[k, step, :, pl.ds(rows, 32), cols], recv2.at[k, step, mine[k], :, :, cols],
+                send2.at[k, sem], rsem2.at[k, sem], n, dev,
+            )
         rows = pl.multiple_of(mine[k] * 32, 32)
-        recv2[k, step, mine[k]] = recv1[k, step, :, pl.ds(rows, 32), :]
-
-    def combine(k, step):
-        take(recv2.at[k, step, pl.ds(0, RING - 1)], rsem2.at[k, step])
-        slots = recv2[k, step].reshape(1024, C)
-        cols = pl.multiple_of(step * C, C)
-        weights = wg[k, :, :, pl.ds(cols, C)].reshape(KS, C)
-        part = dot(gbig[k], slots) + dot(hrecv[k].reshape(RING * TOK, KS), weights)
-        pbuf[k, step] = part.astype(BF).reshape(RING, TOK, C)
+        recv2[k, step, mine[k], :, :, cols] = recv1[k, step, :, pl.ds(rows, 32), cols]
+
+    def combine(k, step, lane, width, sem):
+        cols = pl.ds(lane, width)
+        take(recv2.at[k, step, pl.ds(0, RING - 1), :, :, cols], rsem2.at[k, sem])
+        slots = recv2[k, step, :, :, :, cols].reshape(1024, width)
+        wide = pl.ds(pl.multiple_of(step * WIDE + lane, 128), width)
+        weights = wg[k, :, :, wide].reshape(KS, width)
+        send_part(k, step, lane, width, sem, dot(gbig[k], slots) + dot(hrecv[k].reshape(RING * TOK, KS), weights))
+
+    def send_part(k, step, lane, width, sem, part):
+        cols = pl.ds(lane, width)
+        pbuf[k, step, :, :, cols] = part.astype(BF).reshape(RING, TOK, width)
         own = mine[1 - k]
         for hop in (1, 3, 2):
             to, dev = along(1 - k, hop)
-            remote(pbuf.at[k, step, to], recv3.at[k, step, own], send3.at[k, step], rsem3.at[k, step], n, dev)
-        recv3[k, step, own] = pbuf[k, step, own]
-
-    def finish(k, step):
-        take(recv3.at[k, step, pl.ds(0, RING - 1)], rsem3.at[k, step])
-        total = recv3[k, step, 0].astype(F32)
+            remote(
+                pbuf.at[k, step, to, :, cols], recv3.at[k, step, own, :, cols],
+                send3.at[k, sem], rsem3.at[k, sem], n, dev,
+            )
+        recv3[k, step, own, :, cols] = pbuf[k, step, own, :, cols]
+
+    def finish(k, step, lane, width, sem, extra=None):
+        cols = pl.ds(lane, width)
+        take(recv3.at[k, step, pl.ds(0, RING - 1), :, cols], rsem3.at[k, sem])
+        total = recv3[k, step, 0, :, cols].astype(F32)
         for j in range(1, RING):
-            total += recv3[k, step, j].astype(F32)
-        out_ref[:, pl.ds(pl.multiple_of(k * HALF + step * C, C), C)] = total.astype(BF)
+            total += recv3[k, step, j, :, cols].astype(F32)
+        if extra is not None:
+            total += extra
+        out_ref[:, pl.ds(pl.multiple_of(k * HALF + step * WIDE + lane, 128), width)] = total.astype(BF)
 
     def stage(i, lag, act):
-        @pl.when((i >= lag) & (i < ROUNDS + lag))
+        @pl.when((i >= lag) & (i < LAST + lag))
+        def _():
+            for k in range(2):
+                act(k, i - lag, 0, WIDE, i - lag)
+
+        @pl.when(i == LAST + lag)
         def _():
             for k in range(2):
                 for h in range(PARTS):
-                    act(k, (i - lag) * PARTS + h)
+                    act(k, LAST, h * C, C, LAST + h)
 
     def loop(i, carry):
         @pl.when(i < ROUNDS)
         def _():
             multiply(i)
 
-        @pl.when(i == 0)
+        stage(i, AHEAD, forward)
+
+        @pl.when((i == 2) | (i == 3))
         def _():
-            set_up()
-            gate_pieces()
-
-        stage(i, AHEAD, forward)
-
-        @pl.when(i == AHEAD + 1)
-        def _():
-            widen_gates()
-
+            x_forward(i - 2)
+
+        pl.when(i == AHEAD)(share_rows)
+        pl.when(i == AHEAD + 1)(widen_gates)
         stage(i, AHEAD + 1, combine)
+        pl.when(i == AHEAD + 2)(widen_x)
+
+        for xr in range(XR):
+            @pl.when(i == AHEAD + 3 + xr)
+            def _():
+                x_combine(xr)
+
+            @pl.when(i == AHEAD + 5 + xr)
+            def _():
+                x_finish(xr)
+
         stage(i, AHEAD + 2, finish)
         return carry
 
-    lax.fori_loop(0, ROUNDS + AHEAD + 2, loop, 0)
+    send_rows()
+    hid_copy.wait()
+    multiply(0)
+    multiply(1)
+    for xr in range(XR):
+        x_multiply(xr)
+    set_up()
+    gate_pieces()
+    lax.fori_loop(2, ROUNDS + AHEAD + 2, loop, 0)
 
     for k in range(2):
         take(hsend.at[k, pl.ds(0, RING - 1)], init_send.at[k])
-        take(wg.at[k, pl.ds(0, RING - 1)], init_send.at[2 + k])
+        take(wg.at[k, pl.ds(0, RING - 1), :, pl.ds(0, QUART)], init_send.at[2 + k])
+        take(wg.at[k, :, :, pl.ds(0, QUART)], init_send.at[6 + k])
         take(gsend.at[k, pl.ds(0, RING - 1)], init_send.at[4 + k])
+        for xr in range(XR):
+            take(xbuf.at[k, xr, pl.ds(0, RING - 1)], xs1.at[k, xr])
+            take(xr2.at[k, xr, pl.ds(0, RING - 1)], xs2.at[k, xr])
+            take(xpart.at[k, xr, pl.ds(0, NODES - 1)], xs3.at[k, xr])
+        for step in range(ROUNDS - SLOTS, LAST):
+            take(obuf.at[step % SLOTS, k, pl.ds(0, NODES - 1)], send1.at[step % SLOTS, k, 0])
         for h in range(PARTS):
-            for place in range(SLOTS):
-                take(obuf.at[place, k, h, pl.ds(0, NODES - 1)], send1.at[place, k, h])
+            cols = pl.ds(h * C, C)
+            take(obuf.at[LAST % SLOTS, k, pl.ds(0, NODES - 1), :, cols], send1.at[LAST % SLOTS, k, h])
+            take(recv2.at[k, LAST, pl.ds(0, RING - 1), :, :, cols], send2.at[k, LAST + h])
+            take(recv3.at[k, LAST, pl.ds(0, RING - 1), :, cols], send3.at[k, LAST + h])
+        for xr in range(XR):
+            take(recv3.at[k, ROUNDS + xr, pl.ds(0, RING - 1)], send3.at[k, ROUNDS + 1 + xr])
+    take(asend.at[pl.ds(0, NODES - 1)], ash)
 
     def drain(step, carry):
         for k in range(2):
@@ -280,7 +440,7 @@
             take(recv3.at[k, step, pl.ds(0, RING - 1)], send3.at[k, step])
         return carry
 
-    lax.fori_loop(0, STEPS, drain, 0)
+    lax.fori_loop(0, LAST, drain, 0)
 
 
 def body(expert_hidden, expert_down, shared_hidden, shared_down, expert_ids, gates):
@@ -298,31 +458,48 @@
             pltpu.VMEM((TOP, TOK), jnp.int32),
             pltpu.VMEM((TOP, TOK), F32),
             pltpu.VMEM((2, 2, EF, WIDE), BF),
-            pltpu.VMEM((SLOTS, 2, PARTS, NODES, 128, C), BF),
-            pltpu.VMEM((2, STEPS, NODES, 128, C), BF),
-            pltpu.VMEM((2, STEPS, RING, NODES, 32, C), BF),
-            pltpu.VMEM((2, STEPS, RING, TOK, C), BF),
-            pltpu.VMEM((2, STEPS, RING, TOK, C), BF),
+            pltpu.VMEM((SLOTS, 2, NODES, 128, WIDE), BF),
+            pltpu.VMEM((2, ROUNDS, NODES, 128, WIDE), BF),
+            pltpu.VMEM((2, ROUNDS, RING, NODES, 32, WIDE), BF),
+            pltpu.VMEM((2, ALL, RING, TOK, WIDE), BF),
+            pltpu.VMEM((2, ALL, RING, TOK, WIDE), BF),
             pltpu.VMEM((2, RING, 96, HALF), BF),
             pltpu.VMEM((2, RING * TOK, 1024), BF),
             pltpu.VMEM((2, RING, TOK, KS), BF),
             pltpu.VMEM((2, RING, TOK, 256), BF),
             pltpu.VMEM((2, RING, TOK, KS), BF),
             pltpu.VMEM((2, RING, TOK, 256), BF),
+            pltpu.VMEM((2, XR, RING, RING, 64, WIDE), BF),
+            pltpu.VMEM((2, XR, RING, RING, 64, WIDE), BF),
+            pltpu.VMEM((2, XR, RING, RING, 64, WIDE), BF),
+            pltpu.VMEM((2, XR, NODES, PACK, WIDE), BF),
+            pltpu.VMEM((2, XR, NODES, PACK, WIDE), BF),
+            pltpu.VMEM((2, NODES * PACK, 1024), BF),
+            pltpu.VMEM((NODES, PACK, EXPERTS), BF),
+            pltpu.VMEM((NODES, PACK, EXPERTS), BF),
+            pltpu.VMEM((TOK, NODES * PACK), BF),
             dma,
             dma((2, 2)),
             dma((5,)),
-            dma((6,)),
-            dma((6,)),
+            dma((8,)),
+            dma((8,)),
             dma((SLOTS, 2, PARTS)),
-            dma((2, STEPS)),
-            dma((2, STEPS)),
-            dma((2, STEPS)),
-            dma((2, STEPS)),
-            dma((2, STEPS)),
+            dma((2, ALL + 1)),
+            dma((2, ALL + 1)),
+            dma((2, ALL + 1)),
+            dma((2, ALL + 1)),
+            dma((2, ALL + 1)),
+            dma((2, XR)),
+            dma((2, XR)),
+            dma((2, XR)),
+            dma((2, XR)),
+            dma((2, XR)),
+            dma((2, XR)),
+            dma,
+            dma,
         ],
         compiler_params=pltpu.CompilerParams(
-            collective_id=0, has_side_effects=True, vmem_limit_bytes=56 * 1024 * 1024
+            collective_id=0, has_side_effects=True, vmem_limit_bytes=60 * 1024 * 1024
         ),
         name="combine",
     )(

time: 139 us -> 128 us (0.921)
  Pallas kernels: 138 us -> 127 us
    pallas_call x1, Pallas kernels: 138 us -> 127 us  [body(): pl.pallas_call(kernel, out_shape=pltpu.VMEM((TOK, D), BF), in_specs=[anyw...]
where the time goes in v3:
time: 128 us
  Pallas kernels  127 us (99%)
    pallas_call x1, Pallas kernels, body(): pl.pallas_call(kernel, out_shape=pltpu.VMEM((TOK, D), BF), in_specs=[anyw...  127 us

profile of v3, /device:TPU:1, one launch (start us, length us, event | category | flops | bytes accessed | tf_op | source)
XLA Modules:
  0.0 128.1 jit_solution(9522493337539666750)
XLA Ops:
  0.0 127.0 %combine.1 = bf16[128,5120]{1,0:T(8,128)(2,1)S(1)} custom-call(bf16[1024,1536]{1,0:T(8,128)(2,1)} %hid_h.1, bf16[1536,5120]{1,0:T(8,128)(2,1)} %bitcast.3, bf16[128,1536]{1,0:T(8,128)(2,1)} %sh_h.1, bf16[96,5120]{1,0:T(8,128)(2,1)} %sd_h.1, s32[6,128]{1,0:T(8,128)} %bitcast.4, f32[6,128]{1,0:T(8,128)} %bitcast.5), custom_call_target="tpu_custom_call" | custom-call | tf_op jit(solution)/shard_map/combine/pallas_call | solution.py:450
  127.0 1.1 copy.8

commit v4 on v3

--- a/solution.py
+++ b/solution.py
@@ -31,7 +31,7 @@
 QUART = HALF // 2
 AHEAD = 3
 SLOTS = AHEAD + 2
-NODE_OFFSETS = ((1, 0), (3, 0), (2, 0), (1, 1), (3, 1), (2, 1), (0, 1))
+NODE_OFFSETS = ((2, 0), (2, 1), (1, 0), (3, 0), (1, 1), (3, 1), (0, 1))
 
 
 def iota(shape, dim):
@@ -108,7 +108,7 @@
         pltpu.make_async_copy(ref, ref, sem).wait()
 
     def send_rows():
-        for step in (1, 3, 2):
+        for step in (2, 1, 3):
             _, dev = along(0, step)
             remote(sd_h.at[:, my_quart(0)], wg.at[0, z, :, my_quart(0)], init_send.at[2], init_recv.at[2], n, dev)
             _, dev = along(1, step)
@@ -125,7 +125,7 @@
         for k in range(2):
             own = mine[1 - k]
             hrecv[k, own] = hsend[k, own]
-            for step in (1, 3, 2):
+            for step in (2, 1, 3):
                 to, dev = along(1 - k, step)
                 remote(hsend.at[k, to], hrecv.at[k, own], init_send.at[k], init_recv.at[k], n, dev)
 
@@ -175,7 +175,7 @@
         for k in range(2):
             own = mine[1 - k]
             grecv[k, own] = gsend[k, own]
-            for step in (1, 3, 2):
+            for step in (2, 1, 3):
                 to, dev = along(1 - k, step)
                 remote(gsend.at[k, to], grecv.at[k, own], init_send.at[4 + k], init_recv.at[4 + k], n, dev)
 
@@ -233,7 +233,7 @@
                             pieces.append(o[at:at + 8])
                 o = jnp.concatenate(pieces, axis=0).astype(BF)
                 xbuf[k, xr, :, :, part * 32:(part + 1) * 32, :] = o.reshape(RING, RING, 32, WIDE)
-            for hop in (1, 3, 2):
+            for hop in (2, 1, 3):
                 to, dev = along(k, hop)
                 remote(xbuf.at[k, xr, to], xr1.at[k, xr, mine[k]], xs1.at[k, xr], xq1.at[k, xr], n, dev)
             xr1[k, xr, mine[k]] = xbuf[k, xr, mine[k]]
@@ -242,7 +242,7 @@
         for k in range(2):
             take(xr1.at[k, xr, pl.ds(0, RING - 1)], xq1.at[k, xr])
             own = mine[1 - k]
-            for hop in (1, 3, 2):
+            for hop in (2, 1, 3):
                 to, dev = along(1 - k, hop)
                 remote(xr1.at[k, xr, :, to], xr2.at[k, xr, own], xs2.at[k, xr], xq2.at[k, xr], n, dev)
             xr2[k, xr, own] = xr1[k, xr, :, own]
@@ -324,7 +324,7 @@
     def forward(k, step, lane, width, sem):
         cols = pl.ds(lane, width)
         take(recv1.at[k, step, pl.ds(0, NODES - 1), :, cols], rsem1.at[k, sem])
-        for hop in (1, 3, 2):
+        for hop in (2, 1, 3):
             to, dev = along(k, hop)
             rows = pl.multiple_of(to * 32, 32)
             remote(
@@ -346,7 +346,7 @@
         cols = pl.ds(lane, width)
         pbuf[k, step, :, :, cols] = part.astype(BF).reshape(RING, TOK, width)
         own = mine[1 - k]
-        for hop in (1, 3, 2):
+        for hop in (2, 1, 3):
             to, dev = along(1 - k, hop)
             remote(
                 pbuf.at[k, step, to, :, cols], recv3.at[k, step, own, :, cols],
@@ -364,12 +364,13 @@
             total += extra
         out_ref[:, pl.ds(pl.multiple_of(k * HALF + step * WIDE + lane, 128), width)] = total.astype(BF)
 
-    def stage(i, lag, act):
+    def bulk(i, lag, act):
         @pl.when((i >= lag) & (i < LAST + lag))
         def _():
             for k in range(2):
                 act(k, i - lag, 0, WIDE, i - lag)
 
+    def last(i, lag, act):
         @pl.when(i == LAST + lag)
         def _():
             for k in range(2):
@@ -381,27 +382,30 @@
         def _():
             multiply(i)
 
-        stage(i, AHEAD, forward)
+        bulk(i, AHEAD, forward)
+        last(i, AHEAD, forward)
 
         @pl.when((i == 2) | (i == 3))
         def _():
             x_forward(i - 2)
 
         pl.when(i == AHEAD)(share_rows)
-        pl.when(i == AHEAD + 1)(widen_gates)
-        stage(i, AHEAD + 1, combine)
-        pl.when(i == AHEAD + 2)(widen_x)
+        pl.when(i == AHEAD + 2)(widen_gates)
+        bulk(i, AHEAD + 2, combine)
+        last(i, AHEAD + 1, combine)
+        pl.when(i == AHEAD + 3)(widen_x)
 
         for xr in range(XR):
             @pl.when(i == AHEAD + 3 + xr)
             def _():
                 x_combine(xr)
 
-            @pl.when(i == AHEAD + 5 + xr)
+            @pl.when(i == AHEAD + 6 + xr)
             def _():
                 x_finish(xr)
 
-        stage(i, AHEAD + 2, finish)
+        bulk(i, AHEAD + 3, finish)
+        last(i, AHEAD + 2, finish)
         return carry
 
     send_rows()

time: 128 us -> 125 us (0.977)
  Pallas kernels: 127 us -> 124 us
    pallas_call x1, Pallas kernels: 127 us -> 124 us  [body(): pl.pallas_call(kernel, out_shape=pltpu.VMEM((TOK, D), BF), in_specs=[anyw...]
where the time goes in v4:
time: 125 us
  Pallas kernels  124 us (99%)
    pallas_call x1, Pallas kernels, body(): pl.pallas_call(kernel, out_shape=pltpu.VMEM((TOK, D), BF), in_specs=[anyw...  124 us

profile of v4, /device:TPU:1, one launch (start us, length us, event | category | flops | bytes accessed | tf_op | source)
XLA Modules:
  0.0 124.6 jit_solution(1588345564739288861)
XLA Ops:
  0.0 123.6 %combine.1 = bf16[128,5120]{1,0:T(8,128)(2,1)S(1)} custom-call(bf16[1024,1536]{1,0:T(8,128)(2,1)} %hid_h.1, bf16[1536,5120]{1,0:T(8,128)(2,1)} %bitcast.3, bf16[128,1536]{1,0:T(8,128)(2,1)} %sh_h.1, bf16[96,5120]{1,0:T(8,128)(2,1)} %sd_h.1, s32[6,128]{1,0:T(8,128)} %bitcast.4, f32[6,128]{1,0:T(8,128)} %bitcast.5), custom_call_target="tpu_custom_call" | custom-call | tf_op jit(solution)/shard_map/combine/pallas_call | solution.py:454
  123.6 1.1 copy.8
